TPU v7x, 32 devices: a whole 2x2x4 slice. The times are simulated.
32 devices in a mesh: patch: 16 (over z, y, x), pair: 2 (over core).
Axes of the slice: x: 2, y: 2, z: 4, core: 2. Of those that a mesh axis runs over, the one named last changes fastest.
Arguments:
- node_latent: bfloat16 [5120, 512], P('patch'), may hold values from -6 to 6
- edge_latent: bfloat16 [65536, 512], P(('patch', 'pair')), may hold values from -6 to 6
- edge_sender: int32 [65536], P(('patch', 'pair')), may hold values from 0 to 255
- edge_receiver: int32 [65536], P(('patch', 'pair')), may hold values from 0 to 319
- edge_count: int32 [32], P(('patch', 'pair')), may hold values from 1 to 2048, 32768 in all
- send_rows: int32 [16, 16, 16], P('patch'), may hold values from 0 to 319
- w_edge: bfloat16 [512, 512], replicated, may hold values from -0.15625 to 0.15625
- w_send: bfloat16 [512, 512], replicated, may hold values from -0.15625 to 0.15625
- w_recv: bfloat16 [512, 512], replicated, may hold values from -0.15625 to 0.15625
- edge_bias: float32 [512], replicated, may hold values from -4 to 4
- edge_out: bfloat16 [512, 512], replicated, may hold values from -0.25 to 0.25
- edge_out_bias: float32 [512], replicated, may hold values from -4 to 4
- edge_gain: float32 [512], replicated, may hold values from 0.25 to 1.75
- edge_offset: float32 [512], replicated, may hold values from -2 to 2
- w_node: bfloat16 [512, 512], replicated, may hold values from -0.1875 to 0.1875
- w_agg: bfloat16 [512, 512], replicated, may hold values from -0.1875 to 0.1875
- node_bias: float32 [512], replicated, may hold values from -4 to 4
- node_out: bfloat16 [512, 512], replicated, may hold values from -0.25 to 0.25
- node_out_bias: float32 [512], replicated, may hold values from -4 to 4
- node_gain: float32 [512], replicated, may hold values from 0.25 to 1.75
- node_offset: float32 [512], replicated, may hold values from -2 to 2
Outputs:
- new_edge: bfloat16 [65536, 512], P(('patch', 'pair'))
- new_node: bfloat16 [5120, 512], P('patch')
Inputs may be any that keep to these rules, and one draw needn't show every extreme that they name: `edge_count`: the valid edges of a device are the first ones of its block; some device's block is full.
All inputs are finite; a program needn't handle non-finite values.
Results may differ from a plain program's by a relative error of at most 0.007.
Values may be sent and summed in bfloat16 or wider, within the bound.
A program may use at most 64 MiB of HBM per device.

v0:
```python
import jax
import jax.numpy as jnp
from jax import lax
from jax.sharding import PartitionSpec as P


def layer_norm(values, gain, offset):
    mean = jnp.mean(values, axis=-1, keepdims=True)
    centered = values - mean
    spread = jnp.mean(centered * centered, axis=-1, keepdims=True)
    return centered * lax.rsqrt(spread + 1e-05) * gain + offset


def node_update(
    rows, summed, w_node, w_agg, node_bias, node_out, node_out_bias, node_gain, node_offset
):
    summed_b = summed.astype(jnp.bfloat16)
    node_pre = (
        jnp.dot(rows, w_node, preferred_element_type=jnp.float32)
        + jnp.dot(summed_b, w_agg, preferred_element_type=jnp.float32)
        + node_bias
    )
    node_hidden = jax.nn.silu(node_pre).astype(jnp.bfloat16)
    node_message = (
        jnp.dot(node_hidden, node_out, preferred_element_type=jnp.float32) + node_out_bias
    )
    return (rows.astype(jnp.float32) + layer_norm(node_message, node_gain, node_offset)).astype(
        jnp.bfloat16
    )


def on_device(
    node_latent,
    edge_latent,
    edge_sender,
    edge_receiver,
    edge_count,
    send_rows,
    w_edge,
    w_send,
    w_recv,
    edge_bias,
    edge_out,
    edge_out_bias,
    edge_gain,
    edge_offset,
    w_node,
    w_agg,
    node_bias,
    node_out,
    node_out_bias,
    node_gain,
    node_offset,
):
    node_rows = node_latent.shape[0]
    edge_rows = edge_latent.shape[0]
    width = node_latent.shape[1]
    send_index = send_rows[0]
    patches = send_index.shape[0]
    slots = send_index.shape[1]
    projected = jnp.dot(node_latent, w_send, preferred_element_type=jnp.float32).astype(
        jnp.bfloat16
    )
    outgoing = projected[send_index]
    arrived = lax.all_to_all(outgoing, "patch", split_axis=0, concat_axis=0, tiled=True)
    send_term = arrived.reshape(patches * slots, width)[edge_sender].astype(jnp.float32)
    recv_projected = jnp.dot(node_latent, w_recv, preferred_element_type=jnp.float32)
    pre = (
        jnp.dot(edge_latent, w_edge, preferred_element_type=jnp.float32)
        + send_term
        + recv_projected[edge_receiver]
        + edge_bias
    )
    hidden = jax.nn.silu(pre).astype(jnp.bfloat16)
    message = jnp.dot(hidden, edge_out, preferred_element_type=jnp.float32) + edge_out_bias
    delta = layer_norm(message, edge_gain, edge_offset).astype(jnp.bfloat16)
    valid = jnp.arange(edge_rows, dtype=jnp.int32) < edge_count[0]
    updated = (edge_latent.astype(jnp.float32) + delta.astype(jnp.float32)).astype(jnp.bfloat16)
    new_edge = jnp.where(valid[:, None], updated, edge_latent)
    node_ids = jnp.arange(node_rows, dtype=jnp.int32)
    onehot = ((edge_receiver[None, :] == node_ids[:, None]) & valid[None, :]).astype(jnp.bfloat16)
    partial_value = jnp.dot(onehot, delta, preferred_element_type=jnp.float32)
    summed = lax.psum(partial_value, "pair")
    new_node = node_update(
        node_latent,
        summed,
        w_node,
        w_agg,
        node_bias,
        node_out,
        node_out_bias,
        node_gain,
        node_offset,
    )
    return (new_edge, new_node)


def solution(mesh):
    placed = (
        P("patch", None),
        P(("patch", "pair"), None),
        P(("patch", "pair")),
        P(("patch", "pair")),
        P(("patch", "pair")),
        P("patch", None, None),
        P(),
        P(),
        P(),
        P(),
        P(),
        P(),
        P(),
        P(),
        P(),
        P(),
        P(),
        P(),
        P(),
        P(),
        P(),
    )
    return jax.shard_map(
        on_device,
        mesh=mesh,
        in_specs=placed,
        out_specs=(P(("patch", "pair"), None), P("patch", None)),
        check_vma=False,
    )
```

profile of v0, /device:TPU:0, one launch (start us, length us, event | category | flops | bytes accessed | tf_op | source)
XLA Modules:
  0.0 68.8 jit_solution(1897686304926497275)
XLA Ops:
  0.6 0.0 copy-start
  0.6 0.0 copy-start.3
  0.7 0.0 copy-start.5
  0.7 0.0 copy-start.7
  0.7 0.8 %compare_select_fusion.2 = s32[16,16,1]{1,0,2:T(8,128)S(1)} fusion(s32[1,16,16]{2,1,0:T(8,128)} %param.26), kind=kLoop, calls=%fused_computation.27 | loop fusion | flops 768 | bytes 2048 | tf_op jit(solution)/shard_map/select_n | solution.py:64
  1.5 0.1 reshape.79
  1.6 1.5 %convolution_convert_fusion = bf16[320,512]{1,0:T(8,128)(2,1)S(1)} fusion(bf16[320,512]{1,0:T(8,128)(2,1)} %param.21, bf16[512,512]{1,0:T(8,128)(2,1)} %param.28), kind=kOutput, calls=%fused_computation.18 | convolution fusion | flops 167936000 | bytes 1179648 | tf_op jit(solution)/shard_map/dot_general | solution.py:61
  3.1 1.9 %gather_fusion = bf16[256,512]{1,0:T(8,128)(2,1)} fusion(bf16[320,512]{1,0:T(8,128)(2,1)S(1)} %convolution_convert_fusion, s32[1024]{0:T(1024)S(1)} %pad_clamp_fusion), kind=kCustom, calls=%fused_computation | custom fusion | bytes 525312 | tf_op jit(solution)/shard_map/gather | solution.py:64
  4.9 8.3 %all-to-all-start = ((bf16[16,16,512]{2,1,0:T(8,128)(2,1)}), bf16[16,16,512]{2,1,0:T(8,128)(2,1)S(1)}, u32[]{:S(2)}, u32[]{:S(2)}) async-start(bf16[16,16,512]{2,1,0:T(8,128)(2,1)} %bitcast.2), calls=%async_computation | async-start | bytes 524288 | tf_op jit(solution)/shard_map/all_to_all | solution.py:65
  13.3 0.3 fusion.17
  13.6 0.0 copy-done.7
  14.3 2.9 %copy.23 = bf16[2048,512]{0,1:T(8,128)(2,1)S(1)} copy(bf16[2048,512]{1,0:T(8,128)(2,1)} %param.22) | data formatting | bytes 4194304 | tf_op args[1]
  17.2 8.8 %gather_fusion.2 = f32[2048,512]{1,0:T(8,128)} fusion(f32[320,512]{1,0:T(8,128)S(1)} %fusion.17, s32[2048]{0:T(1024)S(1)} %fusion.13), kind=kCustom, calls=%fused_computation.2 | custom fusion | bytes 8396800 | tf_op jit(solution)/shard_map/gather | solution.py:71
  26.1 0.7 %fusion.12 = s32[2048]{0:T(1024)S(1)} fusion(s32[2048]{0:T(1024)} %param.23), kind=kLoop, calls=%fused_computation.28 | loop fusion | flops 8192 | bytes 16384 | tf_op jit(solution)/shard_map/gather | solution.py:66
  26.8 2.4 %fusion.18 = f32[320,512]{1,0:T(8,128)} fusion(bf16[320,512]{1,0:T(8,128)(2,1)} %param.21, bf16[512,512]{1,0:T(8,128)(2,1)} %param.35), kind=kOutput, calls=%fused_computation.40 | convolution fusion | flops 167772160 | bytes 1507328 | tf_op jit(solution)/shard_map/dot_general | solution.py:19
  29.1 0.0 all-to-all-done
  29.1 0.0 copy-start.14
  29.2 9.2 %gather_fusion.1 = bf16[2048,512]{1,0:T(8,128)(2,1)} fusion(bf16[256,512]{1,0:T(8,128)(2,1)S(1)} %bitcast.21, s32[2048]{0:T(1024)S(1)} %fusion.12), kind=kCustom, calls=%fused_computation.1 | custom fusion | bytes 4202496 | tf_op jit(solution)/shard_map/gather | solution.py:66
  38.4 0.0 copy-done.14
  38.4 8.5 %add_reduce_fusion = (f32[2048]{0:T(1024)S(1)}, f32[2048,512]{0,1:T(8,128)}) fusion(f32[512]{0:T(512)S(1)} %copy-done.6, bf16[512,512]{1,0:T(8,128)(2,1)S(1)} %copy-done, f32[2048,512]{1,0:T(8,128)} %gather_fusion.2, bf16[2048,512]{1,0:T(8,128)(2,1)} %gather_fusion.1, bf16[2048,512]{1,0:T(8,128)(2,1)} %param.22, bf16[512,512]{1,0:T(8,128)(2,1)S(1)} %copy-done.13, ...), kind=kOutput, calls=%fused_computation.7 | convolution fusion | flops 2159015936 | bytes 13643776 | tf_op jit(solution)/shard_map/dot_general | solution.py:75
  46.9 3.0 %multiply_reduce_fusion = f32[2048]{0:T(1024)S(1)} fusion(f32[2048,512]{0,1:T(8,128)} %get-tuple-element.7, f32[2048]{0:T(1024)S(1)} %broadcast_multiply_fusion, f32[512]{0:T(512)S(1)} %copy-done.6), kind=kLoop, calls=%fused_computation.5 | loop fusion | flops 4192256 | bytes 4212736 | tf_op jit(solution)/shard_map/reduce_sum | solution.py:10
  49.9 0.4 copy-done.1
  50.3 0.0 copy-done.9
  50.3 2.9 %fusion = (bf16[2048,512]{0,1:T(8,128)(2,1)}, bf16[2048,512]{0,1:T(8,128)(2,1)S(1)}) fusion(bf16[2048,512]{0,1:T(8,128)(2,1)S(1)} %copy.23, pred[2048]{0:T(1024)(128)(4,1)S(1)} %iota_compare_fusion.1, f32[512]{0:T(512)S(1)} %copy-done.9, f32[512]{0:T(512)S(1)} %copy-done.10, f32[2048]{0:T(1024)S(1)} %add_rsqrt_fusion, f32[2048]{0:T(1024)S(1)} %broadcast_multiply_fusion, ...), kind=kLoop, calls=%fused_computation.8 | loop fusion | flops 11534336 | bytes 10510336 | tf_op jit(solution)/shard_map/jit(_where)/select_n | solution.py:79
  53.2 0.9 %fusion.2 = f32[320,512]{1,0:T(8,128)S(1)} fusion(bf16[2048,512]{0,1:T(8,128)(2,1)S(1)} %get-tuple-element.5, s32[2048]{0:T(1024)S(1)} %copy-done.8, pred[2048]{0:T(1024)(128)(4,1)S(1)} %iota_compare_fusion.1), kind=kOutput, calls=%fused_computation.11 | convolution fusion | flops 672399360 | bytes 2762752 | tf_op jit(solution)/shard_map/dot_general | solution.py:82
  54.1 0.0 copy-start.2
  54.1 5.8 %all-reduce.1 = bf16[320,512]{1,0:T(8,128)(2,1)} all-reduce(f32[320,512]{1,0:T(8,128)S(1)} %fusion.2), channel_id=1, replica_groups=mesh['patch'=16,'pair'=2] {'pair'}, use_global_device_ids=true, to_apply=%region_2.3 | all-reduce | flops 163840 | bytes 983040 | tf_op jit(solution)/shard_map/psum | solution.py:83
  59.9 0.0 copy-start.12
  59.9 3.0 %fusion.16 = (f32[320]{0:T(512)S(1)}, f32[320,512]{1,0:T(8,128)}) fusion(f32[512]{0:T(512)S(1)} %copy-done.15, bf16[512,512]{1,0:T(8,128)(2,1)} %param.38, f32[320,512]{1,0:T(8,128)} %fusion.18, bf16[512,512]{1,0:T(8,128)(2,1)} %param.36, f32[512]{0:T(512)S(1)} %copy-done.16, bf16[320,512]{1,0:T(8,128)(2,1)} %all-reduce.1), kind=kOutput, calls=%fused_computation.38 | convolution fusion | flops 337018560 | bytes 2692352 | tf_op jit(solution)/shard_map/dot_general | solution.py:25
  62.9 1.3 %multiply_reduce_fusion.1 = f32[320]{0:T(512)S(1)} fusion(f32[320,512]{1,0:T(8,128)} %get-tuple-element.9, f32[320]{0:T(512)S(1)} %broadcast_multiply_fusion.1), kind=kLoop, calls=%fused_computation.20 | loop fusion | flops 491200 | bytes 657920 | tf_op jit(solution)/shard_map/reduce_sum | solution.py:10
  64.3 2.5 %copy.25 = bf16[2048,512]{1,0:T(8,128)(2,1)} copy(bf16[2048,512]{0,1:T(8,128)(2,1)S(1)} %copy-done.2) | data formatting | bytes 4194304
  66.8 2.0 %add_convert_fusion.2 = bf16[320,512]{1,0:T(8,128)(2,1)} fusion(bf16[320,512]{1,0:T(8,128)(2,1)S(1)} %copy-done.4, f32[320,512]{1,0:T(8,128)} %get-tuple-element.9, f32[512]{0:T(512)S(1)} %copy-done.11, f32[512]{0:T(512)S(1)} %copy-done.12, f32[320]{0:T(512)S(1)} %add_rsqrt_fusion.1, f32[320]{0:T(512)S(1)} %broadcast_multiply_fusion.1), kind=kLoop, calls=%fused_computation.19 | loop fusion | flops 1146880 | bytes 1317376 | tf_op jit(solution)/shard_map/convert_element_type | solution.py:27
  (30 shorter events, 0.1 us)
Async XLA Ops:
  0.6 37.7 %copy-start = (bf16[512,512]{1,0:T(8,128)(2,1)S(1)}, bf16[512,512]{1,0:T(8,128)(2,1)}, u32[]{:S(2)}) copy-start(bf16[512,512]{1,0:T(8,128)(2,1)} %param.31) | copy-start | bytes 1572868
  0.6 12.6 %copy-start.3 = (bf16[320,512]{1,0:T(8,128)(2,1)S(1)}, bf16[320,512]{1,0:T(8,128)(2,1)}, u32[]{:S(2)}) copy-start(bf16[320,512]{1,0:T(8,128)(2,1)} %param.21) | copy-start | bytes 983044
  0.7 12.6 %copy-start.5 = (bf16[512,512]{1,0:T(8,128)(2,1)S(1)}, bf16[512,512]{1,0:T(8,128)(2,1)}, u32[]{:S(2)}) copy-start(bf16[512,512]{1,0:T(8,128)(2,1)} %param.29) | copy-start | bytes 1572868
  0.7 12.9 %copy-start.7 = (s32[2048]{0:T(1024)S(1)}, s32[2048]{0:T(1024)}, u32[]{:S(2)}) copy-start(s32[2048]{0:T(1024)} %param.24) | copy-start | bytes 24580
  4.9 24.2 %all-to-all-start = ((bf16[16,16,512]{2,1,0:T(8,128)(2,1)}), bf16[16,16,512]{2,1,0:T(8,128)(2,1)S(1)}, u32[]{:S(2)}, u32[]{:S(2)}) async-start(bf16[16,16,512]{2,1,0:T(8,128)(2,1)} %bitcast.2), calls=%async_computation | async-start | bytes 524288 | tf_op jit(solution)/shard_map/all_to_all | solution.py:65
  29.1 9.2 %copy-start.6 = (f32[512]{0:T(512)S(1)}, f32[512]{0:T(512)}, u32[]{:S(2)}) copy-start(f32[512]{0:T(512)} %param.32) | copy-start | bytes 6148
  29.1 9.2 %copy-start.13 = (bf16[512,512]{1,0:T(8,128)(2,1)S(1)}, bf16[512,512]{1,0:T(8,128)(2,1)}, u32[]{:S(2)}) copy-start(bf16[512,512]{1,0:T(8,128)(2,1)} %param.27) | copy-start | bytes 1572868
  29.1 9.2 %copy-start.14 = (f32[512]{0:T(512)S(1)}, f32[512]{0:T(512)}, u32[]{:S(2)}) copy-start(f32[512]{0:T(512)} %param.30) | copy-start | bytes 6148
  46.9 3.4 %copy-start.1 = (f32[2048,512]{0,1:T(8,128)S(1)}, f32[2048,512]{0,1:T(8,128)}, u32[]{:S(2)}) copy-start(f32[2048,512]{0,1:T(8,128)} %get-tuple-element.7) | copy-start | bytes 12582916
  46.9 3.4 %copy-start.9 = (f32[512]{0:T(512)S(1)}, f32[512]{0:T(512)}, u32[]{:S(2)}) copy-start(f32[512]{0:T(512)} %param.34) | copy-start | bytes 6148
  46.9 3.5 %copy-start.10 = (f32[512]{0:T(512)S(1)}, f32[512]{0:T(512)}, u32[]{:S(2)}) copy-start(f32[512]{0:T(512)} %param.33) | copy-start | bytes 6148
  50.3 2.9 %copy-start.8 = (s32[2048]{0:T(1024)S(1)}, s32[2048]{0:T(1024)}, u32[]{:S(2)}) copy-start(s32[2048]{0:T(1024)} %param.24) | copy-start | bytes 24580
  53.2 6.7 %copy-start.15 = (f32[512]{0:T(512)S(1)}, f32[512]{0:T(512)}, u32[]{:S(2)}) copy-start(f32[512]{0:T(512)} %param.39) | copy-start | bytes 6148
  53.2 6.7 %copy-start.16 = (f32[512]{0:T(512)S(1)}, f32[512]{0:T(512)}, u32[]{:S(2)}) copy-start(f32[512]{0:T(512)} %param.37) | copy-start | bytes 6148
  54.1 10.2 %copy-start.2 = (bf16[2048,512]{0,1:T(8,128)(2,1)S(1)}, bf16[2048,512]{0,1:T(8,128)(2,1)}, u32[]{:S(2)}) copy-start(bf16[2048,512]{0,1:T(8,128)(2,1)} %get-tuple-element.4) | copy-start | bytes 6291460
  59.9 6.9 %copy-start.4 = (bf16[320,512]{1,0:T(8,128)(2,1)S(1)}, bf16[320,512]{1,0:T(8,128)(2,1)}, u32[]{:S(2)}) copy-start(bf16[320,512]{1,0:T(8,128)(2,1)} %param.21) | copy-start | bytes 983044
  59.9 6.9 %copy-start.11 = (f32[512]{0:T(512)S(1)}, f32[512]{0:T(512)}, u32[]{:S(2)}) copy-start(f32[512]{0:T(512)} %param.41) | copy-start | bytes 6148
  59.9 6.9 %copy-start.12 = (f32[512]{0:T(512)S(1)}, f32[512]{0:T(512)}, u32[]{:S(2)}) copy-start(f32[512]{0:T(512)} %param.40) | copy-start | bytes 6148
where the time goes:
time: 69.4 us; the launch traced here: 68.8 us
  local copies, waits for them, and re-layouts  25.9 us (37%)
  matrix products  16.5 us (24%)
  other arithmetic  10.7 us (15%)
  starting transfers between devices  8.34 us (12%)
  blocking collectives  5.79 us (8%)
  between operations  1.47 us (2%)
    gather x1, local copies, waits for them, and re-layouts, on_device(): arrived.reshape(patches * slots, width)[edge_sender].astype(jnp.float32)  9.21 us
    gather x1, local copies, waits for them, and re-layouts, on_device(): recv_projected[edge_receiver]  8.84 us
    dot_general x1, matrix products, on_device(): jnp.dot(hidden, edge_out, preferred_element_type=jnp.float32)  8.47 us
    all_to_all x1, starting transfers between devices, on_device(): lax.all_to_all(outgoing, 'patch', split_axis=0, concat_axis=0, tiled=True)  8.34 us
    unnamed x36, local copies, waits for them, and re-layouts  5.96 us
    psum x1, blocking collectives, on_device(): summed = lax.psum(partial_value, 'pair')  5.79 us
    reduce_sum x2, other arithmetic, layer_norm(): spread = jnp.mean(centered * centered, axis=-1, keepdims=True)  4.29 us
    dot_general x1, matrix products, node_update(): jnp.dot(node_hidden, node_out, preferred_element_type=jnp.float32)  3.04 us
  transfers between devices with their start and end apart: 1, of which 0 were waited for; matrix products, arithmetic and copies ran while one was open for 22% of the time, Pallas kernels for 0%

commit v1 on v0

v1 whole, which is shorter than its diff:
```python
import functools

import jax
import jax.numpy as jnp
from jax import lax
from jax.experimental import pallas as pl
from jax.experimental.pallas import tpu as pltpu
from jax.sharding import PartitionSpec as P

MESH = pl.DeviceIdType.MESH
LANES = 128
F32 = jnp.float32
BF16 = jnp.bfloat16
EPS = 1e-05


def round_up(count, unit):
    return (count + unit - 1) // unit * unit


def dot(left, right):
    return jnp.dot(left, right, preferred_element_type=F32)


def silu(values):
    half = 0.5 * values
    return half + half * jnp.tanh(half)


def layer_norm(values, gain, offset):
    scale = 1.0 / values.shape[-1]
    mean = jnp.sum(values, axis=-1, keepdims=True) * scale
    centered = values - mean
    spread = jnp.sum(centered * centered, axis=-1, keepdims=True) * scale
    return centered * lax.rsqrt(spread + EPS) * gain + offset


def onehot_rows(row, width):
    blocks = []
    for start in range(0, row.shape[1], LANES):
        piece = row[:, start : start + LANES]
        column = jnp.transpose(jnp.broadcast_to(piece, (LANES, LANES)))
        lane = lax.broadcasted_iota(jnp.int32, (LANES, LANES), 1)
        parts = [
            jnp.where(column == lane + first, 1.0, 0.0).astype(BF16)
            for first in range(0, width, LANES)
        ]
        blocks.append(jnp.concatenate(parts, axis=1))
    return jnp.concatenate(blocks, axis=0)


def kernel(
    patches,
    tile,
    early,
    count_ref,
    send_rows_ref,
    sender_ref,
    receiver_ref,
    edge_bias_ref,
    edge_out_bias_ref,
    edge_gain_ref,
    edge_offset_ref,
    node_bias_ref,
    node_out_bias_ref,
    node_gain_ref,
    node_offset_ref,
    node_hbm,
    edge_hbm,
    w_edge_hbm,
    w_send_hbm,
    w_recv_hbm,
    edge_out_hbm,
    w_node_hbm,
    w_agg_hbm,
    node_out_hbm,
    new_edge_hbm,
    new_node_ref,
    node,
    edges,
    first_table,
    w_send,
    w_recv,
    edge_out,
    w_node,
    w_agg,
    node_out,
    outgoing,
    arrived,
    send_table,
    part,
    send_hot,
    recv_hot,
    updated,
    aggregate,
    agg_mine,
    agg_other,
    node_part,
    load_sem,
    edge_sem,
    store_sem,
    send_sem,
    recv_sem,
    pass_sem,
    passed_sem,
    agg_sem,
):
    me = lax.axis_index("patch")
    core = lax.axis_index("pair")
    other = 1 - core
    nodes, width = node_hbm.shape
    padded = node.shape[0]
    edge_rows = edge_hbm.shape[0]
    tiles = edge_rows // tile
    slots, half = outgoing.shape[1:]
    barrier = pltpu.get_barrier_semaphore()

    def greet(step, carry):
        pl.semaphore_signal(
            barrier, inc=1, device_id=(lax.rem(me + step, patches), core), device_id_type=MESH
        )
        return carry

    lax.fori_loop(1, patches, greet, 0)
    pl.semaphore_signal(barrier, inc=1, device_id=(me, other), device_id_type=MESH)

    loads = [
        pltpu.make_async_copy(source, target, load_sem.at[number])
        for number, (source, target) in enumerate(
            (
                (node_hbm, node.at[pl.ds(0, nodes)]),
                (w_recv_hbm, w_recv),
                (w_edge_hbm, first_table.at[pl.ds(0, width)]),
                (w_node_hbm, w_node),
                (w_send_hbm, w_send),
                (edge_out_hbm, edge_out),
                (w_agg_hbm, w_agg),
                (node_out_hbm, node_out),
            )
        )
    ]

    def edge_load(index):
        rows = pl.ds(index * tile, tile)
        return pltpu.make_async_copy(edge_hbm.at[rows], edges.at[rows], edge_sem.at[index])

    for load in loads[:3]:
        load.start()
    for index in range(tiles):
        edge_load(index).start()
    for load in loads[3:]:
        load.start()

    if padded > nodes:
        node[pl.ds(nodes, padded - nodes), :] = jnp.zeros((padded - nodes, width), BF16)
    loads[0].wait()
    columns = pl.ds(pl.multiple_of(core * half, LANES), half)
    block = max(1, LANES // slots)
    for first in range(0, patches, block):
        hot = onehot_rows(send_rows_ref[:, first * slots : (first + block) * slots], padded)
        picked = dot(hot, node[:, columns]).astype(BF16)
        outgoing[first : first + block] = picked.reshape(block, slots, half)

    loads[1].wait()
    first_table[pl.ds(width, padded), :] = dot(node[...], w_recv[...]).astype(BF16)
    loads[2].wait()

    def first_layer(index, carry):
        rows = pl.ds(pl.multiple_of(index * tile, tile), tile)
        edge_load(index).wait()
        receiver = receiver_ref[:, rows]
        hot = onehot_rows(receiver, padded)
        left = jnp.concatenate([edges[rows, :], hot], axis=1)
        part[rows, :] = dot(left, first_table[...]) + edge_bias_ref[...]
        send_hot[rows, :] = onehot_rows(sender_ref[:, rows], send_hot.shape[1])
        ids = lax.broadcasted_iota(jnp.int32, (nodes, tile), 0)
        recv_hot[:, rows] = jnp.where(ids == receiver, 1.0, 0.0).astype(BF16)
        return carry

    lax.fori_loop(0, early, first_layer, 0)

    pl.semaphore_wait(barrier, patches)

    def to_patch(step):
        target = lax.rem(me + step, patches)
        return pltpu.make_async_remote_copy(
            src_ref=outgoing.at[target],
            dst_ref=arrived.at[core, me],
            send_sem=send_sem.at[target],
            recv_sem=recv_sem.at[me],
            device_id=(target, core),
            device_id_type=MESH,
        )

    def from_patch(source):
        return pltpu.make_async_remote_copy(
            src_ref=outgoing.at[source],
            dst_ref=arrived.at[core, source],
            send_sem=send_sem.at[source],
            recv_sem=recv_sem.at[source],
            device_id=(source, core),
            device_id_type=MESH,
        )

    def to_core(source, source_ref):
        return pltpu.make_async_remote_copy(
            src_ref=source_ref,
            dst_ref=arrived.at[core, source],
            send_sem=pass_sem.at[source],
            recv_sem=passed_sem.at[source],
            device_id=(me, other),
            device_id_type=MESH,
        )

    def from_core(source):
        return pltpu.make_async_remote_copy(
            src_ref=arrived.at[core, source],
            dst_ref=arrived.at[other, source],
            send_sem=pass_sem.at[source],
            recv_sem=passed_sem.at[source],
            device_id=(me, other),
            device_id_type=MESH,
        )

    def send_step(step, carry):
        to_patch(step).start()
        return carry

    lax.fori_loop(1, patches, send_step, 0)
    to_core(me, outgoing.at[me]).start()
    arrived[core, me] = outgoing[me]

    lax.fori_loop(early, tiles, first_layer, 0)

    for load in loads[3:]:
        load.wait()
    node_part[...] = dot(node[pl.ds(0, nodes), :], w_node[...]) + node_bias_ref[...]
    aggregate[...] = jnp.zeros_like(aggregate)

    def pass_step(step, carry):
        source = lax.rem(me + patches - step, patches)
        from_patch(source).wait_recv()
        to_core(source, arrived.at[core, source]).start()
        return carry

    lax.fori_loop(1, patches, pass_step, 0)

    def passed_step(step, carry):
        from_core(lax.rem(me + patches - step, patches)).wait_recv()
        return carry

    lax.fori_loop(0, patches, passed_step, 0)
    for first in range(0, patches, block):
        rows = jnp.concatenate(
            [arrived[side, first : first + block].reshape(block * slots, half) for side in range(2)],
            axis=1,
        )
        send_table[first * slots : (first + block) * slots, :] = dot(rows, w_send[...]).astype(BF16)

    count = count_ref[0]

    def store(index):
        rows = pl.ds(pl.multiple_of(index * tile, tile), tile)
        return pltpu.make_async_copy(updated.at[rows], new_edge_hbm.at[rows], store_sem.at[index])

    def second_layer(index, carry):
        rows = pl.ds(pl.multiple_of(index * tile, tile), tile)
        pre = part[rows, :] + dot(send_hot[rows, :], send_table[...])
        hidden = silu(pre).astype(BF16)
        message = dot(hidden, edge_out[...]) + edge_out_bias_ref[...]
        delta = layer_norm(message, edge_gain_ref[...], edge_offset_ref[...])
        ids = lax.broadcasted_iota(jnp.int32, (tile, width), 0) + index * tile
        delta = jnp.where(ids < count, delta, 0.0).astype(BF16)
        updated[rows, :] = (edges[rows, :].astype(F32) + delta.astype(F32)).astype(BF16)
        store(index).start()
        aggregate[...] += dot(recv_hot[:, rows], delta)
        return carry

    lax.fori_loop(0, tiles, second_layer, 0)

    agg_mine[...] = aggregate[...].astype(BF16)
    exchange = pltpu.make_async_remote_copy(
        src_ref=agg_mine,
        dst_ref=agg_other,
        send_sem=agg_sem.at[0],
        recv_sem=agg_sem.at[1],
        device_id=(me, other),
        device_id_type=MESH,
    )
    exchange.start()

    def sent_step(step, carry):
        to_patch(step).wait_send()
        source = lax.rem(me + step, patches)
        to_core(source, arrived.at[core, source]).wait_send()
        return carry

    lax.fori_loop(1, patches, sent_step, 0)
    to_core(me, outgoing.at[me]).wait_send()
    exchange.wait()

    summed = (agg_mine[...].astype(F32) + agg_other[...].astype(F32)).astype(BF16)
    hidden = silu(node_part[...] + dot(summed, w_agg[...])).astype(BF16)
    message = dot(hidden, node_out[...]) + node_out_bias_ref[...]
    normed = layer_norm(message, node_gain_ref[...], node_offset_ref[...])
    new_node_ref[...] = (node[pl.ds(0, nodes), :].astype(F32) + normed).astype(BF16)

    def stored_step(index, carry):
        store(index).wait()
        return carry

    lax.fori_loop(0, tiles, stored_step, 0)


def on_device(
    patches,
    node_latent,
    edge_latent,
    edge_sender,
    edge_receiver,
    edge_count,
    send_rows,
    w_edge,
    w_send,
    w_recv,
    edge_bias,
    edge_out,
    edge_out_bias,
    edge_gain,
    edge_offset,
    w_node,
    w_agg,
    node_bias,
    node_out,
    node_out_bias,
    node_gain,
    node_offset,
):
    nodes, width = node_latent.shape
    edge_rows = edge_latent.shape[0]
    slots = send_rows.shape[2]
    senders = patches * slots
    padded = round_up(nodes, LANES)
    half = width // 2
    tile = 256
    early = 2
    tiles = edge_rows // tile
    vmem = pl.BlockSpec(memory_space=pltpu.VMEM)
    smem = pl.BlockSpec(memory_space=pltpu.SMEM)
    hbm = pl.BlockSpec(memory_space=pl.ANY)
    weight = pltpu.VMEM((width, width), BF16)
    return pl.pallas_call(
        functools.partial(kernel, patches, tile, early),
        out_shape=(
            jax.ShapeDtypeStruct(edge_latent.shape, BF16),
            jax.ShapeDtypeStruct(node_latent.shape, BF16),
        ),
        in_specs=[smem] + [vmem] * 11 + [hbm] * 9,
        out_specs=(hbm, vmem),
        scratch_shapes=[
            pltpu.VMEM((padded, width), BF16),
            pltpu.VMEM((edge_rows, width), BF16),
            pltpu.VMEM((width + padded, width), BF16),
            weight,
            weight,
            weight,
            weight,
            weight,
            weight,
            pltpu.VMEM((patches, slots, half), BF16),
            pltpu.VMEM((2, patches, slots, half), BF16),
            pltpu.VMEM((senders, width), BF16),
            pltpu.VMEM((edge_rows, width), F32),
            pltpu.VMEM((edge_rows, senders), BF16),
            pltpu.VMEM((nodes, edge_rows), BF16),
            pltpu.VMEM((edge_rows, width), BF16),
            pltpu.VMEM((nodes, width), F32),
            pltpu.VMEM((nodes, width), BF16),
            pltpu.VMEM((nodes, width), BF16),
            pltpu.VMEM((nodes, width), F32),
            pltpu.SemaphoreType.DMA((8,)),
            pltpu.SemaphoreType.DMA((tiles,)),
            pltpu.SemaphoreType.DMA((tiles,)),
            pltpu.SemaphoreType.DMA((patches,)),
            pltpu.SemaphoreType.DMA((patches,)),
            pltpu.SemaphoreType.DMA((patches,)),
            pltpu.SemaphoreType.DMA((patches,)),
            pltpu.SemaphoreType.DMA((2,)),
        ],
        compiler_params=pltpu.CompilerParams(
            collective_id=0, has_side_effects=True, vmem_limit_bytes=60 * 1024 * 1024
        ),
    )(
        edge_count,
        send_rows.reshape(1, senders),
        edge_sender.reshape(1, edge_rows),
        edge_receiver.reshape(1, edge_rows),
        edge_bias.reshape(1, width),
        edge_out_bias.reshape(1, width),
        edge_gain.reshape(1, width),
        edge_offset.reshape(1, width),
        node_bias.reshape(1, width),
        node_out_bias.reshape(1, width),
        node_gain.reshape(1, width),
        node_offset.reshape(1, width),
        node_latent,
        edge_latent,
        w_edge,
        w_send,
        w_recv,
        edge_out,
        w_node,
        w_agg,
        node_out,
    )


def solution(mesh):
    placed = (
        P("patch", None),
        P(("patch", "pair"), None),
        P(("patch", "pair")),
        P(("patch", "pair")),
        P(("patch", "pair")),
        P("patch", None, None),
    ) + (P(),) * 15
    return jax.shard_map(
        functools.partial(on_device, mesh.shape["patch"]),
        mesh=mesh,
        in_specs=placed,
        out_specs=(P(("patch", "pair"), None), P("patch", None)),
        check_vma=False,
    )
```

time: 69.4 us -> 31.5 us (0.45)
  Pallas kernels: 0 us -> 24.8 us
  local copies, waits for them, and re-layouts: 25.9 us -> 5.16 us
  matrix products: 16.5 us -> 0 us
  other arithmetic: 10.7 us -> 0 us
  starting transfers between devices: 8.34 us -> 0 us
  blocking collectives: 5.79 us -> 0 us
    pallas_call x0 -> x1, Pallas kernels: none -> 24.8 us  [on_device(): pl.pallas_call(functools.partial(kernel, patches, tile, early), out_shape...]
    gather x3 -> x0, local copies, waits for them, and re-layouts: 19.9 us -> none  [the longest x1 9.21 us: on_device(): arrived.reshape(patches * slots, width)[edge_sender].astype(jnp.float32)]
    dot_general x6 -> x0, matrix products: 16.5 us -> none  [the longest x1 8.47 us: on_device(): jnp.dot(hidden, edge_out, preferred_element_type=jnp.float32)]
    all_to_all x1 -> x0, starting transfers between devices: 8.34 us -> none  [on_device(): lax.all_to_all(outgoing, 'patch', split_axis=0, concat_axis=0, tiled=True)]
    psum x1 -> x0, blocking collectives: 5.79 us -> none  [on_device(): summed = lax.psum(partial_value, 'pair')]
    reduce_sum x2 -> x0, other arithmetic: 4.29 us -> none  [layer_norm(): spread = jnp.mean(centered * centered, axis=-1, keepdims=True)]
    select_n x2 -> x0, other arithmetic: 3.67 us -> none  [the longest x1 2.87 us: on_device(): new_edge = jnp.where(valid[:, None], updated, edge_latent)]
    unnamed x36 -> x4, local copies, waits for them, and re-layouts: 5.96 us -> 3.82 us
  transfers between devices with their start and end apart: 1 -> 0, of which waited for: 0 -> 0; matrix products, arithmetic and copies ran while one was open for 22% -> 0% of each run, Pallas kernels for 0% -> 0%
where the time goes in v1:
time: 31.5 us; the launch traced here: 31.2 us
  Pallas kernels  24.8 us (79%)
  local copies, waits for them, and re-layouts  5.16 us (16%)
  between operations  1.29 us (4%)
    pallas_call x1, Pallas kernels, on_device(): pl.pallas_call(functools.partial(kernel, patches, tile, early), out_shape...  24.8 us
    unnamed x4, local copies, waits for them, and re-layouts  3.82 us
    reshape x1, local copies, waits for them, and re-layouts, on_device(): send_rows.reshape(1, senders)  1.34 us

profile of v1, /device:TPU:0, one launch (start us, length us, event | category | flops | bytes accessed | tf_op | source)
XLA Modules:
  0.0 31.2 jit_solution(9316311594443324517)
XLA Ops:
  1.3 1.3 %reshape.37.send_rows_ref = s32[1,256]{1,0:T(1,128)} reshape(s32[1,16,16]{2,1,0:T(8,128)} %param.26) | data formatting | bytes 2048 | tf_op jit(solution)/shard_map/reshape | solution.py:395
  2.6 24.8 %shard_map.212 = (bf16[2048,512]{1,0:T(8,128)(2,1)}, bf16[320,512]{1,0:T(8,128)(2,1)}) custom-call(s32[1]{0:T(128)S(6)} %copy.25.count_ref, s32[1,256]{1,0:T(1,128)} %reshape.37.send_rows_ref, s32[1,2048]{1,0:T(1,128)} %bitcast.10, s32[1,2048]{1,0:T(1,128)} %bitcast.11, f32[1,512]{1,0:T(1,128)} %bitcast.12, f32[1,512]{1,0:T(1,128)} %bitcast.13, ...), custom_call_target="tpu_custom_call" | custom-call | tf_op jit(solution)/shard_map/pallas_call | solution.py:352
  27.4 0.0 copy-start
  27.4 3.1 %copy.26 = bf16[2048,512]{1,0:T(8,128)(2,1)} copy(bf16[2048,512]{1,0:T(8,128)(2,1)} %get-tuple-element.4) | data formatting | bytes 4194304
  30.5 0.0 copy-done
  30.5 0.7 %copy.27 = bf16[320,512]{1,0:T(8,128)(2,1)} copy(bf16[320,512]{1,0:T(8,128)(2,1)S(1)} %copy-done) | data formatting | bytes 655360
Async XLA Ops:
  27.4 3.1 %copy-start = (bf16[320,512]{1,0:T(8,128)(2,1)S(1)}, bf16[320,512]{1,0:T(8,128)(2,1)}, u32[]{:S(2)}) copy-start(bf16[320,512]{1,0:T(8,128)(2,1)} %get-tuple-element.5) | copy-start | bytes 983044

commit v2 on v1

--- a/solution.py
+++ b/solution.py
@@ -49,11 +49,45 @@
     return jnp.concatenate(blocks, axis=0)
 
 
-def kernel(
+def onehot_slots(rows, width):
+    count, slots = rows.shape
+    eye = lax.broadcasted_iota(jnp.int32, (slots, slots), 0) == lax.broadcasted_iota(
+        jnp.int32, (slots, slots), 1
+    )
+    picked = [
+        jnp.where(eye, jnp.broadcast_to(rows[at : at + 1], (slots, slots)), 0)
+        for at in range(count)
+    ]
+    column = jnp.sum(jnp.concatenate(picked, axis=0).astype(F32), axis=1, keepdims=True)
+    lane = lax.broadcasted_iota(jnp.int32, (count * slots, LANES), 1).astype(F32)
+    return jnp.concatenate(
+        [jnp.where(column == lane + first, 1.0, 0.0).astype(BF16) for first in range(0, width, LANES)],
+        axis=1,
+    )
+
+
+def edge_kernel(
     patches,
     tile,
     early,
+    chunk,
+    pieces,
     count_ref,
+    send_rows_hbm,
+    sender_hbm,
+    receiver_hbm,
+    edge_bias_hbm,
+    edge_out_bias_hbm,
+    edge_gain_hbm,
+    edge_offset_hbm,
+    node_hbm,
+    edge_hbm,
+    w_edge_hbm,
+    w_send_hbm,
+    w_recv_hbm,
+    edge_out_hbm,
+    new_edge_hbm,
+    summed_ref,
     send_rows_ref,
     sender_ref,
     receiver_ref,
@@ -61,30 +95,12 @@
     edge_out_bias_ref,
     edge_gain_ref,
     edge_offset_ref,
-    node_bias_ref,
-    node_out_bias_ref,
-    node_gain_ref,
-    node_offset_ref,
-    node_hbm,
-    edge_hbm,
-    w_edge_hbm,
-    w_send_hbm,
-    w_recv_hbm,
-    edge_out_hbm,
-    w_node_hbm,
-    w_agg_hbm,
-    node_out_hbm,
-    new_edge_hbm,
-    new_node_ref,
     node,
     edges,
     first_table,
     w_send,
     w_recv,
     edge_out,
-    w_node,
-    w_agg,
-    node_out,
     outgoing,
     arrived,
     send_table,
@@ -95,7 +111,6 @@
     aggregate,
     agg_mine,
     agg_other,
-    node_part,
     load_sem,
     edge_sem,
     store_sem,
@@ -115,55 +130,69 @@
     slots, half = outgoing.shape[1:]
     barrier = pltpu.get_barrier_semaphore()
 
-    def greet(step, carry):
-        pl.semaphore_signal(
-            barrier, inc=1, device_id=(lax.rem(me + step, patches), core), device_id_type=MESH
-        )
-        return carry
-
-    lax.fori_loop(1, patches, greet, 0)
-    pl.semaphore_signal(barrier, inc=1, device_id=(me, other), device_id_type=MESH)
-
     loads = [
         pltpu.make_async_copy(source, target, load_sem.at[number])
         for number, (source, target) in enumerate(
             (
                 (node_hbm, node.at[pl.ds(0, nodes)]),
+                (send_rows_hbm, send_rows_ref),
                 (w_recv_hbm, w_recv),
                 (w_edge_hbm, first_table.at[pl.ds(0, width)]),
-                (w_node_hbm, w_node),
+                (sender_hbm, sender_ref),
+                (receiver_hbm, receiver_ref),
+                (edge_bias_hbm, edge_bias_ref),
                 (w_send_hbm, w_send),
                 (edge_out_hbm, edge_out),
-                (w_agg_hbm, w_agg),
-                (node_out_hbm, node_out),
+                (edge_out_bias_hbm, edge_out_bias_ref),
+                (edge_gain_hbm, edge_gain_ref),
+                (edge_offset_hbm, edge_offset_ref),
             )
         )
     ]
+    for load in loads[:2]:
+        load.start()
+
+    def far_first(at, ends):
+        low, high = ends
+        take_low = me - low > high - me
+        target = jnp.where(take_low, low, high)
+        return target, (jnp.where(take_low, low + 1, low), jnp.where(take_low, high, high - 1))
+
+    def greet(at, ends):
+        target, ends = far_first(at, ends)
+        pl.semaphore_signal(barrier, inc=1, device_id=(target, core), device_id_type=MESH)
+        return ends
+
+    ends = (jnp.int32(0), jnp.int32(patches - 1))
+    lax.fori_loop(1, patches, greet, ends)
+    pl.semaphore_signal(barrier, inc=1, device_id=(me, other), device_id_type=MESH)
 
     def edge_load(index):
         rows = pl.ds(index * tile, tile)
         return pltpu.make_async_copy(edge_hbm.at[rows], edges.at[rows], edge_sem.at[index])
 
-    for load in loads[:3]:
+    for load in loads[2:7]:
         load.start()
     for index in range(tiles):
         edge_load(index).start()
-    for load in loads[3:]:
+    for load in loads[7:]:
         load.start()
 
     if padded > nodes:
         node[pl.ds(nodes, padded - nodes), :] = jnp.zeros((padded - nodes, width), BF16)
     loads[0].wait()
+    loads[1].wait()
     columns = pl.ds(pl.multiple_of(core * half, LANES), half)
     block = max(1, LANES // slots)
     for first in range(0, patches, block):
-        hot = onehot_rows(send_rows_ref[:, first * slots : (first + block) * slots], padded)
+        hot = onehot_slots(send_rows_ref[first : first + block, :], padded)
         picked = dot(hot, node[:, columns]).astype(BF16)
         outgoing[first : first + block] = picked.reshape(block, slots, half)
 
-    loads[1].wait()
+    loads[2].wait()
     first_table[pl.ds(width, padded), :] = dot(node[...], w_recv[...]).astype(BF16)
-    loads[2].wait()
+    for load in loads[3:7]:
+        load.wait()
 
     def first_layer(index, carry):
         rows = pl.ds(pl.multiple_of(index * tile, tile), tile)
@@ -181,8 +210,7 @@
 
     pl.semaphore_wait(barrier, patches)
 
-    def to_patch(step):
-        target = lax.rem(me + step, patches)
+    def to_patch(target):
         return pltpu.make_async_remote_copy(
             src_ref=outgoing.at[target],
             dst_ref=arrived.at[core, me],
@@ -222,19 +250,19 @@
             device_id_type=MESH,
         )
 
-    def send_step(step, carry):
-        to_patch(step).start()
-        return carry
-
-    lax.fori_loop(1, patches, send_step, 0)
+    def send_step(at, ends):
+        target, ends = far_first(at, ends)
+        to_patch(target).start()
+        return ends
+
+    lax.fori_loop(1, patches, send_step, ends)
     to_core(me, outgoing.at[me]).start()
     arrived[core, me] = outgoing[me]
 
     lax.fori_loop(early, tiles, first_layer, 0)
 
-    for load in loads[3:]:
+    for load in loads[7:]:
         load.wait()
-    node_part[...] = dot(node[pl.ds(0, nodes), :], w_node[...]) + node_bias_ref[...]
     aggregate[...] = jnp.zeros_like(aggregate)
 
     def pass_step(step, carry):
@@ -260,23 +288,30 @@
     count = count_ref[0]
 
     def store(index):
-        rows = pl.ds(pl.multiple_of(index * tile, tile), tile)
+        rows = pl.ds(pl.multiple_of(index * chunk, chunk), chunk)
         return pltpu.make_async_copy(updated.at[rows], new_edge_hbm.at[rows], store_sem.at[index])
 
     def second_layer(index, carry):
-        rows = pl.ds(pl.multiple_of(index * tile, tile), tile)
-        pre = part[rows, :] + dot(send_hot[rows, :], send_table[...])
-        hidden = silu(pre).astype(BF16)
-        message = dot(hidden, edge_out[...]) + edge_out_bias_ref[...]
-        delta = layer_norm(message, edge_gain_ref[...], edge_offset_ref[...])
-        ids = lax.broadcasted_iota(jnp.int32, (tile, width), 0) + index * tile
-        delta = jnp.where(ids < count, delta, 0.0).astype(BF16)
-        updated[rows, :] = (edges[rows, :].astype(F32) + delta.astype(F32)).astype(BF16)
+        span = chunk // pieces
+        deltas = []
+        for piece in range(pieces):
+            first = pl.multiple_of(index * chunk, chunk) + piece * span
+            rows = pl.ds(first, span)
+            pre = part[rows, :] + dot(send_hot[rows, :], send_table[...])
+            hidden = silu(pre).astype(BF16)
+            message = dot(hidden, edge_out[...]) + edge_out_bias_ref[...]
+            delta = layer_norm(message, edge_gain_ref[...], edge_offset_ref[...])
+            ids = lax.broadcasted_iota(jnp.int32, (span, width), 0) + first
+            delta = jnp.where(ids < count, delta, 0.0).astype(BF16)
+            updated[rows, :] = (edges[rows, :].astype(F32) + delta.astype(F32)).astype(BF16)
+            deltas.append(delta)
         store(index).start()
-        aggregate[...] += dot(recv_hot[:, rows], delta)
+        rows = pl.ds(pl.multiple_of(index * chunk, chunk), chunk)
+        aggregate[...] += dot(recv_hot[:, rows], jnp.concatenate(deltas, axis=0))
         return carry
 
-    lax.fori_loop(0, tiles, second_layer, 0)
+    chunks = edge_rows // chunk
+    lax.fori_loop(0, chunks, second_layer, 0)
 
     agg_mine[...] = aggregate[...].astype(BF16)
     exchange = pltpu.make_async_remote_copy(
@@ -290,26 +325,86 @@
     exchange.start()
 
     def sent_step(step, carry):
-        to_patch(step).wait_send()
         source = lax.rem(me + step, patches)
+        to_patch(source).wait_send()
         to_core(source, arrived.at[core, source]).wait_send()
         return carry
 
     lax.fori_loop(1, patches, sent_step, 0)
     to_core(me, outgoing.at[me]).wait_send()
-    exchange.wait()
-
-    summed = (agg_mine[...].astype(F32) + agg_other[...].astype(F32)).astype(BF16)
-    hidden = silu(node_part[...] + dot(summed, w_agg[...])).astype(BF16)
-    message = dot(hidden, node_out[...]) + node_out_bias_ref[...]
-    normed = layer_norm(message, node_gain_ref[...], node_offset_ref[...])
-    new_node_ref[...] = (node[pl.ds(0, nodes), :].astype(F32) + normed).astype(BF16)
 
     def stored_step(index, carry):
         store(index).wait()
         return carry
 
-    lax.fori_loop(0, tiles, stored_step, 0)
+    lax.fori_loop(0, chunks, stored_step, 0)
+    exchange.wait()
+    summed_ref[...] = (agg_mine[...].astype(F32) + agg_other[...].astype(F32)).astype(BF16)
+
+
+def node_kernel(
+    pieces,
+    node_bias_ref,
+    node_out_bias_ref,
+    node_gain_ref,
+    node_offset_ref,
+    summed_hbm,
+    node_hbm,
+    w_node_hbm,
+    w_agg_hbm,
+    node_out_hbm,
+    edge_hbm,
+    new_edge_hbm,
+    new_node_ref,
+    summed,
+    node,
+    w_node,
+    w_agg,
+    node_out,
+    edges,
+    load_sem,
+    in_sem,
+    out_sem,
+):
+    rows = edge_hbm.shape[0] // pieces
+    loads = [
+        pltpu.make_async_copy(source, target, load_sem.at[number])
+        for number, (source, target) in enumerate(
+            (
+                (node_hbm, node),
+                (w_node_hbm, w_node),
+                (summed_hbm, summed),
+                (w_agg_hbm, w_agg),
+                (node_out_hbm, node_out),
+            )
+        )
+    ]
+    takes = [
+        pltpu.make_async_copy(
+            edge_hbm.at[pl.ds(at * rows, rows)], edges.at[pl.ds(at * rows, rows)], in_sem.at[at]
+        )
+        for at in range(pieces)
+    ]
+    puts = [
+        pltpu.make_async_copy(
+            edges.at[pl.ds(at * rows, rows)], new_edge_hbm.at[pl.ds(at * rows, rows)], out_sem.at[at]
+        )
+        for at in range(pieces)
+    ]
+    for copy in takes + loads:
+        copy.start()
+    for take, put in zip(takes, puts):
+        take.wait()
+        put.start()
+    for load in loads:
+        load.wait()
+    node_pre = dot(node[...], w_node[...]) + dot(summed[...], w_agg[...]) + node_bias_ref[...]
+    hidden = silu(node_pre).astype(BF16)
+    message = dot(hidden, node_out[...]) + node_out_bias_ref[...]
+    normed = layer_norm(message, node_gain_ref[...], node_offset_ref[...])
+    new_node_ref[...] = (node[...].astype(F32) + normed).astype(BF16)
+    for put in puts:
+        put.wait()
 
 
 def on_device(
@@ -344,74 +439,114 @@
     half = width // 2
     tile = 256
     early = 2
+    chunk = 512
+    pieces = 1
     tiles = edge_rows // tile
     vmem = pl.BlockSpec(memory_space=pltpu.VMEM)
     smem = pl.BlockSpec(memory_space=pltpu.SMEM)
     hbm = pl.BlockSpec(memory_space=pl.ANY)
     weight = pltpu.VMEM((width, width), BF16)
-    return pl.pallas_call(
-        functools.partial(kernel, patches, tile, early),
+    vector = pltpu.VMEM((1, width), F32)
+    scratch = [
+        pltpu.VMEM((patches, slots), jnp.int32),
+        pltpu.VMEM((1, edge_rows), jnp.int32),
+        pltpu.VMEM((1, edge_rows), jnp.int32),
+        vector,
+        vector,
+        vector,
+        vector,
+        pltpu.VMEM((padded, width), BF16),
+        pltpu.VMEM((edge_rows, width), BF16),
+        pltpu.VMEM((width + padded, width), BF16),
+        weight,
+        weight,
+        weight,
+        pltpu.VMEM((patches, slots, half), BF16),
+        pltpu.VMEM((2, patches, slots, half), BF16),
+        pltpu.VMEM((senders, width), BF16),
+        pltpu.VMEM((edge_rows, width), F32),
+        pltpu.VMEM((edge_rows, senders), BF16),
+        pltpu.VMEM((nodes, edge_rows), BF16),
+        pltpu.VMEM((edge_rows, width), BF16),
+        pltpu.VMEM((nodes, width), F32),
+        pltpu.VMEM((nodes, width), BF16),
+        pltpu.VMEM((nodes, width), BF16),
+    ]
+    edge_flops = 2 * edge_rows * width * (2 * width + senders + padded + nodes)
+    edge_new, summed = pl.pallas_call(
+        functools.partial(edge_kernel, patches, tile, early, chunk, pieces),
         out_shape=(
             jax.ShapeDtypeStruct(edge_latent.shape, BF16),
             jax.ShapeDtypeStruct(node_latent.shape, BF16),
         ),
-        in_specs=[smem] + [vmem] * 11 + [hbm] * 9,
+        in_specs=[smem] + [hbm] * 13,
         out_specs=(hbm, vmem),
-        scratch_shapes=[
-            pltpu.VMEM((padded, width), BF16),
-            pltpu.VMEM((edge_rows, width), BF16),
-            pltpu.VMEM((width + padded, width), BF16),
-            weight,
-            weight,
-            weight,
-            weight,
-            weight,
-            weight,
-            pltpu.VMEM((patches, slots, half), BF16),
-            pltpu.VMEM((2, patches, slots, half), BF16),
-            pltpu.VMEM((senders, width), BF16),
-            pltpu.VMEM((edge_rows, width), F32),
-            pltpu.VMEM((edge_rows, senders), BF16),
-            pltpu.VMEM((nodes, edge_rows), BF16),
-            pltpu.VMEM((edge_rows, width), BF16),
-            pltpu.VMEM((nodes, width), F32),
-            pltpu.VMEM((nodes, width), BF16),
-            pltpu.VMEM((nodes, width), BF16),
-            pltpu.VMEM((nodes, width), F32),
-            pltpu.SemaphoreType.DMA((8,)),
+        scratch_shapes=scratch
+        + [
+            pltpu.SemaphoreType.DMA((12,)),
             pltpu.SemaphoreType.DMA((tiles,)),
-            pltpu.SemaphoreType.DMA((tiles,)),
+            pltpu.SemaphoreType.DMA((edge_rows // chunk,)),
             pltpu.SemaphoreType.DMA((patches,)),
             pltpu.SemaphoreType.DMA((patches,)),
             pltpu.SemaphoreType.DMA((patches,)),
             pltpu.SemaphoreType.DMA((patches,)),
             pltpu.SemaphoreType.DMA((2,)),
         ],
+        cost_estimate=pl.CostEstimate(
+            flops=edge_flops, bytes_accessed=4 * edge_rows * width, transcendentals=0
+        ),
         compiler_params=pltpu.CompilerParams(
-            collective_id=0, has_side_effects=True, vmem_limit_bytes=60 * 1024 * 1024
+            collective_id=0, has_side_effects=True, vmem_limit_bytes=62 * 1024 * 1024
         ),
     )(
         edge_count,
-        send_rows.reshape(1, senders),
+        send_rows.reshape(patches, slots),
         edge_sender.reshape(1, edge_rows),
         edge_receiver.reshape(1, edge_rows),
         edge_bias.reshape(1, width),
         edge_out_bias.reshape(1, width),
         edge_gain.reshape(1, width),
         edge_offset.reshape(1, width),
-        node_bias.reshape(1, width),
-        node_out_bias.reshape(1, width),
-        node_gain.reshape(1, width),
-        node_offset.reshape(1, width),
         node_latent,
         edge_latent,
         w_edge,
         w_send,
         w_recv,
         edge_out,
+    )
+    node_pieces = 4
+    rows = pltpu.VMEM((nodes, width), BF16)
+    return pl.pallas_call(
+        functools.partial(node_kernel, node_pieces),
+        out_shape=(
+            jax.ShapeDtypeStruct(edge_latent.shape, BF16),
+            jax.ShapeDtypeStruct(node_latent.shape, BF16),
+        ),
+        in_specs=[vmem] * 4 + [hbm] * 6,
+        out_specs=(hbm, vmem),
+        scratch_shapes=[
+            rows,
+            rows,
+            weight,
+            weight,
+            weight,
+            pltpu.VMEM((edge_rows, width), BF16),
+            pltpu.SemaphoreType.DMA((5,)),
+            pltpu.SemaphoreType.DMA((node_pieces,)),
+            pltpu.SemaphoreType.DMA((node_pieces,)),
+        ],
+        compiler_params=pltpu.CompilerParams(vmem_limit_bytes=60 * 1024 * 1024),
+    )(
+        node_bias.reshape(1, width),
+        node_out_bias.reshape(1, width),
+        node_gain.reshape(1, width),
+        node_offset.reshape(1, width),
+        summed,
+        node_latent,
         w_node,
         w_agg,
         node_out,
+        edge_new,
     )
 
 

time: 31.5 us -> 27.7 us (0.88)
  local copies, waits for them, and re-layouts: 5.16 us -> 0 us
  Pallas kernels: 24.8 us -> 26.2 us
    unnamed x4 -> x0, local copies, waits for them, and re-layouts: 3.82 us -> none
    pallas_call x1 -> x2, Pallas kernels: 24.8 us -> 26.2 us  [the longest x1 21.2 us: on_device(): pl.pallas_call(functools.partial(edge_kernel, patches, tile, early, chunk...]
    reshape x1 -> x0, local copies, waits for them, and re-layouts: 1.34 us -> none  [on_device(): send_rows.reshape(1, senders)]
where the time goes in v2:
time: 27.7 us; the launch traced here: 27.5 us
  Pallas kernels  26.2 us (95%)
  between operations  1.29 us (5%)
    pallas_call x1, Pallas kernels, on_device(): pl.pallas_call(functools.partial(edge_kernel, patches, tile, early, chunk...  21.2 us
    pallas_call x1, Pallas kernels, on_device(): pl.pallas_call(functools.partial(node_kernel, node_pieces), out_shape=(ja...  5 us

profile of v2, /device:TPU:0, one launch (start us, length us, event | category | flops | bytes accessed | tf_op | source)
XLA Modules:
  0.0 27.5 jit_solution(18330135593574764250)
XLA Ops:
  1.3 21.2 %shard_map.212 = (bf16[2048,512]{1,0:T(8,128)(2,1)}, bf16[320,512]{1,0:T(8,128)(2,1)}) custom-call(s32[1]{0:T(128)S(6)} %copy.23.count_ref, s32[16,16]{1,0:T(8,128)} %bitcast.15, s32[1,2048]{1,0:T(1,128)} %bitcast.16, s32[1,2048]{1,0:T(1,128)} %bitcast.17, f32[1,512]{1,0:T(1,128)} %bitcast.18, f32[1,512]{1,0:T(1,128)} %bitcast.19, f32[1,512]{1,0:T(1,128)} %bitcast.20, ...), custom_call_target="tpu_custom_call" | custom-call | flops 4160749568 | bytes 4194304 | tf_op jit(solution)/shard_map/pallas_call | solution.py:476
  22.5 5.0 %shard_map.213 = (bf16[2048,512]{1,0:T(8,128)(2,1)}, bf16[320,512]{1,0:T(8,128)(2,1)}) custom-call(f32[1,512]{1,0:T(1,128)} %bitcast.11, f32[1,512]{1,0:T(1,128)} %bitcast.12, f32[1,512]{1,0:T(1,128)} %bitcast.13, f32[1,512]{1,0:T(1,128)} %bitcast.14, bf16[320,512]{1,0:T(8,128)(2,1)} %get-tuple-element.4.summed_hbm, bf16[320,512]{1,0:T(8,128)(2,1)} %node_hbm.3, ...), custom_call_target="tpu_custom_call" | custom-call | tf_op jit(solution)/shard_map/pallas_call | solution.py:519

commit v3 on v2

--- a/solution.py
+++ b/solution.py
@@ -69,7 +69,6 @@
 def edge_kernel(
     patches,
     tile,
-    early,
     chunk,
     pieces,
     count_ref,
@@ -189,10 +188,6 @@
         picked = dot(hot, node[:, columns]).astype(BF16)
         outgoing[first : first + block] = picked.reshape(block, slots, half)
 
-    loads[2].wait()
-    first_table[pl.ds(width, padded), :] = dot(node[...], w_recv[...]).astype(BF16)
-    for load in loads[3:7]:
-        load.wait()
 
     def first_layer(index, carry):
         rows = pl.ds(pl.multiple_of(index * tile, tile), tile)
@@ -206,8 +201,6 @@
         recv_hot[:, rows] = jnp.where(ids == receiver, 1.0, 0.0).astype(BF16)
         return carry
 
-    lax.fori_loop(0, early, first_layer, 0)
-
     pl.semaphore_wait(barrier, patches)
 
     def to_patch(target):
@@ -259,7 +252,11 @@
     to_core(me, outgoing.at[me]).start()
     arrived[core, me] = outgoing[me]
 
-    lax.fori_loop(early, tiles, first_layer, 0)
+    loads[2].wait()
+    first_table[pl.ds(width, padded), :] = dot(node[...], w_recv[...]).astype(BF16)
+    for load in loads[3:7]:
+        load.wait()
+    lax.fori_loop(0, tiles, first_layer, 0)
 
     for load in loads[7:]:
         load.wait()
@@ -391,7 +388,7 @@
         )
         for at in range(pieces)
     ]
-    for copy in takes + loads:
+    for copy in loads + takes:
         copy.start()
     for take, put in zip(takes, puts):
         take.wait()
@@ -438,7 +435,6 @@
     padded = round_up(nodes, LANES)
     half = width // 2
     tile = 256
-    early = 2
     chunk = 512
     pieces = 1
     tiles = edge_rows // tile
@@ -474,7 +470,7 @@
     ]
     edge_flops = 2 * edge_rows * width * (2 * width + senders + padded + nodes)
     edge_new, summed = pl.pallas_call(
-        functools.partial(edge_kernel, patches, tile, early, chunk, pieces),
+        functools.partial(edge_kernel, patches, tile, chunk, pieces),
         out_shape=(
             jax.ShapeDtypeStruct(edge_latent.shape, BF16),
             jax.ShapeDtypeStruct(node_latent.shape, BF16),

time: 27.7 us -> 27.4 us (0.989)
  no operation moved by 1% of the time
where the time goes in v3:
time: 27.4 us; the launch traced here: 27.3 us
  Pallas kernels  26 us (95%)
  between operations  1.29 us (5%)
    pallas_call x1, Pallas kernels, on_device(): pl.pallas_call(functools.partial(edge_kernel, patches, tile, chunk, piece...  21.2 us
    pallas_call x1, Pallas kernels, on_device(): pl.pallas_call(functools.partial(node_kernel, node_pieces), out_shape=(ja...  4.78 us

profile of v3, /device:TPU:0, one launch (start us, length us, event | category | flops | bytes accessed | tf_op | source)
XLA Modules:
  0.0 27.3 jit_solution(17908163117077789780)
XLA Ops:
  1.3 21.2 %shard_map.212 = (bf16[2048,512]{1,0:T(8,128)(2,1)}, bf16[320,512]{1,0:T(8,128)(2,1)}) custom-call(s32[1]{0:T(128)S(6)} %copy.23.count_ref, s32[16,16]{1,0:T(8,128)} %bitcast.15, s32[1,2048]{1,0:T(1,128)} %bitcast.16, s32[1,2048]{1,0:T(1,128)} %bitcast.17, f32[1,512]{1,0:T(1,128)} %bitcast.18, f32[1,512]{1,0:T(1,128)} %bitcast.19, f32[1,512]{1,0:T(1,128)} %bitcast.20, ...), custom_call_target="tpu_custom_call" | custom-call | flops 4160749568 | bytes 4194304 | tf_op jit(solution)/shard_map/pallas_call | solution.py:472
  22.5 4.8 %shard_map.213 = (bf16[2048,512]{1,0:T(8,128)(2,1)}, bf16[320,512]{1,0:T(8,128)(2,1)}) custom-call(f32[1,512]{1,0:T(1,128)} %bitcast.11, f32[1,512]{1,0:T(1,128)} %bitcast.12, f32[1,512]{1,0:T(1,128)} %bitcast.13, f32[1,512]{1,0:T(1,128)} %bitcast.14, bf16[320,512]{1,0:T(8,128)(2,1)} %get-tuple-element.4.summed_hbm, bf16[320,512]{1,0:T(8,128)(2,1)} %node_hbm.3, ...), custom_call_target="tpu_custom_call" | custom-call | tf_op jit(solution)/shard_map/pallas_call | solution.py:515
